TPU v7x, 32 devices: a whole 2x2x4 slice. The times are simulated.
32 devices in a mesh: tp: 4 (over z), dp: 8 (over y, x, core).
Axes of the slice: x: 2, y: 2, z: 4, core: 2. Of those that a mesh axis runs over, the one named last changes fastest.
Arguments:
- hidden: bfloat16 [8, 1024, 768], P('dp')
- ln_gamma: float32 [768], replicated
- ln_beta: float32 [768], replicated
- embed_table: bfloat16 [50272, 768], P('tp')
- labels: int32 [8, 1024], P('dp')
- loss_mask: int32 [8, 1024], P('dp')
Outputs:
- output 1: float32 [], replicated
- output 2: bfloat16 [8, 1024, 768], P('dp')
- output 3: float32 [50272, 768], P('tp')
- output 4: float32 [768], replicated
- output 5: float32 [768], replicated
All inputs are finite; a program needn't handle non-finite values.
Results may differ from a plain program's by a relative error of at most 0.001.
Values sent between devices are 32-bit elements.
A program may use at most 1 GiB of HBM per device.

v0:
```python
import jax
import jax.numpy as jnp
from jax import lax
from jax.sharding import PartitionSpec as P

LAYER_EPS = 1e-5


def layer_norm_fwd(hidden, ln_gamma, ln_beta):
    x_float = hidden.astype(jnp.float32)
    row_mean = jnp.mean(x_float, axis=-1, keepdims=True)
    centered = x_float - row_mean
    inv_std = lax.rsqrt(jnp.mean(centered * centered, axis=-1, keepdims=True) + LAYER_EPS)
    x_hat = centered * inv_std
    normed = (x_hat * ln_gamma + ln_beta).astype(jnp.bfloat16)
    return x_hat, inv_std, normed


def layer_norm_bwd(grad_normed, x_hat, inv_std, ln_gamma):
    grad_scaled = grad_normed * ln_gamma
    grad_x = (grad_scaled - jnp.mean(grad_scaled, axis=-1, keepdims=True) - x_hat * jnp.mean(grad_scaled * x_hat, axis=-1, keepdims=True)) * inv_std
    return grad_x.astype(jnp.bfloat16)


def solution(mesh):
    def local_step(hidden, ln_gamma, ln_beta, embed_shard, labels, loss_mask):
        shard_rows = embed_shard.shape[0]
        shard_start = lax.axis_index('tp') * shard_rows
        x_hat, inv_std, normed = layer_norm_fwd(hidden, ln_gamma, ln_beta)
        logits = jnp.einsum('bsd,vd->bsv', normed, embed_shard, preferred_element_type=jnp.float32)
        row_max = lax.pmax(jnp.max(logits, axis=-1, keepdims=True), 'tp')
        shifted = jnp.exp(logits - row_max)
        exp_sum = lax.psum(jnp.sum(shifted, axis=-1, keepdims=True), 'tp')
        vocab_ids = lax.broadcasted_iota(jnp.int32, (1, 1, shard_rows), 2) + shard_start
        is_target = vocab_ids == labels[..., None]
        target_logit = lax.psum(jnp.sum(jnp.where(is_target, logits, 0.0), axis=-1, keepdims=True), 'tp')
        log_norm = row_max + jnp.log(exp_sum)
        mask_float = loss_mask.astype(jnp.float32)[..., None]
        token_count = lax.psum(jnp.sum(mask_float), 'dp')
        mean_loss = lax.psum(jnp.sum(mask_float * (log_norm - target_logit)), 'dp') / token_count
        soft_probs = shifted / exp_sum
        grad_logits = (jnp.where(is_target, soft_probs - 1.0, soft_probs) * (mask_float / token_count)).astype(jnp.bfloat16)
        grad_normed = lax.psum(jnp.einsum('bsv,vd->bsd', grad_logits, embed_shard, preferred_element_type=jnp.float32), 'tp')
        d_embed = lax.psum(jnp.einsum('bsv,bsd->vd', grad_logits, normed, preferred_element_type=jnp.float32), 'dp')
        d_gamma = lax.psum(jnp.sum(grad_normed * x_hat, axis=(0, 1)), 'dp')
        d_beta = lax.psum(jnp.sum(grad_normed, axis=(0, 1)), 'dp')
        d_hidden = layer_norm_bwd(grad_normed, x_hat, inv_std, ln_gamma)
        return mean_loss, d_hidden, d_embed, d_gamma, d_beta

    return jax.shard_map(local_step, mesh=mesh, in_specs=(P('dp', None, None), P(None), P(None), P('tp', None), P('dp', None), P('dp', None)), out_specs=(P(), P('dp', None, None), P('tp', None), P(None), P(None)), check_vma=False)
```

profile of v0, /device:TPU:0, one launch (start us, length us, event | category | flops | bytes accessed | tf_op | source)
XLA Modules:
  0.0 773.2 jit_solution(9792805337457139244)
XLA Ops:
  7.2 0.0 all-reduce.5.cloned.1.call-start
  7.2 1.4 convert_reduce_fusion.1
  8.7 15.8 %psum.59 = f32[]{:T(128)} all-reduce(f32[]{:T(128)} %convert_reduce_fusion.1), channel_id=1, replica_groups=mesh['tp'=4,'dp'=8] {'dp'}, use_global_device_ids=true, to_apply=%region_11.12 | all-reduce | flops 1 | bytes 8 | tf_op jit(solution)/shard_map/psum | solution.py:39
  24.5 1.3 convert_divide_fusion
  25.8 1.7 convert_reduce_fusion
  27.5 2.0 fusion.17
  29.6 38.1 %fusion.24 = (f32[1024]{0:T(1024)S(1)}, f32[1024,12568]{0,1:T(8,128)}) fusion(bf16[12568,768]{1,0:T(8,128)(2,1)} %param.9, bf16[1,1024,768]{2,1,0:T(8,128)(2,1)S(1)} %copy-done, f32[768]{0:T(1024)S(1)} %copy-done.4, f32[768]{0:T(1024)S(1)} %copy-done.3, f32[1024]{0:T(1024)S(1)} %add_rsqrt_fusion, f32[1024]{0:T(1024)S(1)} %broadcast_multiply_fusion.2), kind=kOutput, calls=%fused_computation.37 | convolution fusion | flops 19785342976 | bytes 72374272 | tf_op jit(solution)/shard_map/bsd,vd->bsv/dot_general | solution.py:30
  67.6 11.9 %pmax.7 = f32[1,1024,1]{1,2,0:T(1,128)S(1)} all-reduce(f32[1,1024,1]{1,2,0:T(1,128)S(1)} %bitcast.31), channel_id=1, replica_groups=mesh['tp'=4,'dp'=8] {'tp'}, use_global_device_ids=true, to_apply=%region_3.0 | all-reduce | flops 1024 | bytes 8192 | tf_op jit(solution)/shard_map/pmax | solution.py:31
  79.6 22.3 %fusion.3 = (f32[1024]{0:T(1024)S(1)}, f32[1024]{0:T(1024)S(1)}) fusion(f32[1024,12568]{0,1:T(8,128)} %get-tuple-element.17, f32[1024]{0:T(1024)S(1)} %bitcast.23, s32[1024]{0:T(1024)S(1)} %bitcast.25, s32[12568]{0:T(1024)S(1)} %iota_add_fusion), kind=kLoop, calls=%fused_computation.6 | loop fusion | flops 64346112 | bytes 51545184 | tf_op jit(solution)/shard_map/reduce_sum | solution.py:33
  101.8 8.5 %all-reduce.1 = (f32[1,1024,1]{1,2,0:T(1,128)S(1)}, f32[1,1024,1]{1,2,0:T(1,128)S(1)}) all-reduce(f32[1,1024,1]{1,2,0:T(1,128)S(1)} %bitcast.29, f32[1,1024,1]{1,2,0:T(1,128)S(1)} %bitcast.28), channel_id=1, replica_groups=mesh['tp'=4,'dp'=8] {'tp'}, use_global_device_ids=true, to_apply=%region_7.8 | all-reduce | flops 2048 | bytes 16384 | tf_op jit(solution)/shard_map/psum | solution.py:36
  110.4 26.3 %fusion.2 = bf16[1024,12568]{0,1:T(8,128)(2,1)} fusion(f32[1024,12568]{0,1:T(8,128)} %get-tuple-element.17, f32[1024]{0:T(1024)S(1)} %bitcast.27, f32[1024]{0:T(1024)S(1)} %bitcast.30, s32[1024]{0:T(1024)S(1)} %bitcast.26, f32[1024]{0:T(1024)S(1)} %bitcast.24, s32[12568]{0:T(1024)S(1)} %iota_add_fusion), kind=kLoop, calls=%fused_computation.4 | loop fusion | flops 90087424 | bytes 77284448 | tf_op jit(solution)/shard_map/convert_element_type | solution.py:42
  136.6 27.9 %convolution_bitcast_fusion = f32[1,1024,768]{2,1,0:T(8,128)} fusion(bf16[1024,12568]{0,1:T(8,128)(2,1)} %fusion.2, bf16[12568,768]{1,0:T(8,128)(2,1)} %param.9), kind=kOutput, calls=%fused_computation.24 | convolution fusion | flops 19767754752 | bytes 48189440 | tf_op jit(solution)/shard_map/bsv,vd->bsd/dot_general | solution.py:43
  164.6 0.0 all-reduce.5.cloned.1.call-update
  164.6 0.2 all-reduce.7.cloned.1.call-start
  164.8 30.7 %fusion.20 = f32[12568,768]{1,0:T(8,128)} fusion(bf16[1024,12568]{0,1:T(8,128)(2,1)} %fusion.2, bf16[1,1024,768]{2,1,0:T(8,128)(2,1)S(1)} %copy-done, f32[768]{0:T(1024)S(1)} %copy-done.4, f32[768]{0:T(1024)S(1)} %copy-done.3, f32[1024]{0:T(1024)S(1)} %add_rsqrt_fusion, f32[1024]{0:T(1024)S(1)} %broadcast_multiply_fusion.2), kind=kOutput, calls=%fused_computation.35 | convolution fusion | flops 19772473344 | bytes 65935360 | tf_op jit(solution)/shard_map/bsv,bsd->vd/dot_general | solution.py:44
  195.5 0.0 all-reduce.7.cloned.1.call-update
  195.5 0.7 copy-done.1
  196.2 0.6 fusion.19
  196.8 85.6 %all-reduce.5.cloned.1.call-done = f32[1,1024,768]{2,1,0:T(8,128)} async-done(((f32[1,1024,768]{2,1,0:T(8,128)}), f32[1,1024,768]{2,1,0:T(8,128)}) %all-reduce.5.cloned.1.call-update) | async-done | bytes 3145744 | tf_op jit(solution)/shard_map/psum | solution.py:43
  282.4 3.1 fusion.16
  285.4 14.9 %all-reduce = (f32[]{:T(128)}, f32[768]{0:T(1024)}, f32[768]{0:T(1024)}) all-reduce(f32[]{:T(128)} %fusion.19, f32[768]{0:T(1024)S(1)} %get-tuple-element.7, f32[768]{0:T(1024)S(1)} %get-tuple-element.10), channel_id=1, replica_groups=mesh['tp'=4,'dp'=8] {'dp'}, use_global_device_ids=true, to_apply=%region_9.10 | all-reduce | flops 1537 | bytes 12296 | tf_op jit(solution)/shard_map/psum | solution.py:40
  301.7 3.5 fusion.15
  305.2 432.8 %all-reduce.7.cloned.1.call-done = f32[12568,768]{1,0:T(8,128)} async-done(((f32[12568,768]{1,0:T(8,128)}), f32[12568,768]{1,0:T(8,128)}) %all-reduce.7.cloned.1.call-update) | async-done | bytes 38608912 | tf_op jit(solution)/shard_map/psum | solution.py:44
  738.0 27.3 %copy.13 = f32[12568,768]{1,0:T(8,128)} copy(f32[12568,768]{1,0:T(8,128)} %all-reduce.7.cloned.1.call-done) | data formatting | bytes 77217792
  (13 shorter events, 0.0 us)
Async XLA Ops:
  7.2 22.4 %copy-start = (bf16[1,1024,768]{2,1,0:T(8,128)(2,1)S(1)}, bf16[1,1024,768]{2,1,0:T(8,128)(2,1)}, u32[]{:S(2)}) copy-start(bf16[1,1024,768]{2,1,0:T(8,128)(2,1)} %param.6) | copy-start | bytes 4718596
  7.2 22.4 %copy-start.3 = (f32[768]{0:T(1024)S(1)}, f32[768]{0:T(1024)}, u32[]{:S(2)}) copy-start(f32[768]{0:T(1024)} %param.7) | copy-start | bytes 9220
  7.2 22.4 %copy-start.4 = (f32[768]{0:T(1024)S(1)}, f32[768]{0:T(1024)}, u32[]{:S(2)}) copy-start(f32[768]{0:T(1024)} %param.8) | copy-start | bytes 9220
  7.2 275.2 %all-reduce.5.cloned.1.call-start = ((), (), s32[]{:S(2)}) async-start(), calls=%async_computation | async-start | bytes 6291456 | tf_op jit(solution)/shard_map/psum | solution.py:43
  29.6 50.0 %copy-start.2 = (s32[1,1024]{1,0:T(1,128)S(1)}, s32[1,1024]{1,0:T(1,128)}, u32[]{:S(2)}) copy-start(s32[1,1024]{1,0:T(1,128)} %param.10) | copy-start | bytes 12292
  164.6 573.4 %all-reduce.7.cloned.1.call-start = ((), (), s32[]{:S(2)}) async-start(), calls=%async_computation.1 | async-start | bytes 77217792 | tf_op jit(solution)/shard_map/psum | solution.py:44
  195.5 0.7 copy-start.1
Sparse Core Ops, SparseCore 0:
  164.7 117.6 all-reduce.4
  286.7 451.2 all-reduce.6
where the time goes:
time: 774 us; the launch traced here: 773 us
  waiting for transfers between devices  518 us (67%)
  matrix products  96.7 us (12%)
  other arithmetic  62.2 us (8%)
  blocking collectives  51.2 us (7%)
  local copies, waits for them, and re-layouts  28 us (4%)
  between operations  16.6 us (2%)
    psum x1, waiting for transfers between devices, local_step(): lax.psum(jnp.einsum('bsv,bsd->vd', grad_logits, normed, preferred_element...  433 us
    psum x1, waiting for transfers between devices, local_step(): lax.psum(jnp.einsum('bsv,vd->bsd', grad_logits, embed_shard, preferred_el...  85.6 us
    dot_general x1, matrix products, local_step(): jnp.einsum('bsd,vd->bsv', normed, embed_shard, preferred_element_type=jnp...  38.1 us
    dot_general x1, matrix products, local_step(): jnp.einsum('bsv,bsd->vd', grad_logits, normed, preferred_element_type=jnp...  30.7 us
    unnamed x11, local copies, waits for them, and re-layouts  28 us
    dot_general x1, matrix products, local_step(): jnp.einsum('bsv,vd->bsd', grad_logits, embed_shard, preferred_element_typ...  27.9 us
    convert_element_type x1, other arithmetic, local_step(): (jnp.where(is_target, soft_probs - 1.0, soft_probs) * (mask_float / token...  26.3 us
    reduce_sum x1, other arithmetic, local_step(): exp_sum = lax.psum(jnp.sum(shifted, axis=-1, keepdims=True), 'tp')  22.3 us
  transfers between devices with their start and end apart: 2, of which 2 were waited for; matrix products, arithmetic and copies ran while one was open for 5% of the time, Pallas kernels for 0%

commit v1 on v0

v1 whole, which is shorter than its diff:
```python
import jax
import jax.numpy as jnp
from jax import lax
from jax.experimental import pallas as pl
from jax.experimental.pallas import tpu as pltpu
from jax.sharding import PartitionSpec as P

LAYER_EPS = 1e-5
MESH = pl.DeviceIdType.MESH
F32, BF16 = jnp.float32, jnp.bfloat16
SEQ, WIDTH = 1024, 768
ROWS = 12568
BLOCK = 512
FULL = ROWS // BLOCK
REST = ROWS - FULL * BLOCK
RESTPAD = 384
CHUNK = 256
HALF = 512
A_ROWS, A_STEPS = 256, 4
B_ROWS, B_STEPS = 272, 8
A_TOTAL = 8 * A_ROWS * A_STEPS
TAIL = ROWS - A_TOTAL - 2 * B_ROWS * B_STEPS
TAIL_AT = ROWS - TAIL
R_MAX = B_ROWS + TAIL
VMEM_LIMIT = 67_043_328


def layer_norm_fwd(hidden, ln_gamma, ln_beta):
    x_float = hidden.astype(F32)
    row_mean = jnp.mean(x_float, axis=-1, keepdims=True)
    centered = x_float - row_mean
    inv_std = lax.rsqrt(jnp.mean(centered * centered, axis=-1, keepdims=True) + LAYER_EPS)
    x_hat = centered * inv_std
    return x_hat, inv_std, x_hat * ln_gamma + ln_beta


class Plane:
    def __init__(self):
        self.me = me = lax.axis_index('dp')
        self.core = lax.rem(me, 2)
        dx = 2 - 4 * lax.rem(lax.div(me, 2), 2)
        dy = 4 - 8 * lax.div(me, 4)
        self.x, self.y, self.diag = me + dx, me + dy, me + dx + dy
        self.pair = p = me + 1 - 2 * self.core
        self.pair_x, self.pair_y, self.pair_diag = p + dx, p + dy, p + dx + dy


class Gather:
    def __init__(self, plane, region, send_sems, recv_sems):
        self.p, self.region, self.s, self.r = plane, region, send_sems, recv_sems

    def copy(self, lane, q, src, dst, device):
        return pltpu.make_async_remote_copy(
            src_ref=src, dst_ref=dst, send_sem=self.s.at[lane, q], recv_sem=self.r.at[lane, q],
            device_id={'dp': device}, device_id_type=MESH)

    def pass_on(self, lane, q, owner, device):
        part = self.region(owner, q)
        self.copy(lane, q, part, part, device).start()

    def arrived(self, lane, q, owner):
        part = self.region(owner, q)
        self.copy(lane, q, part, part, self.p.pair).wait_recv()

    def sent(self, lane, q, owner):
        part = self.region(owner, q)
        self.copy(lane, q, part, part, self.p.pair).wait_send()

    def send_own(self, q, src):
        p = self.p
        for lane, device in ((1, p.x), (2, p.y), (0, p.pair)):
            self.copy(lane, q, src, self.region(p.me, q), device).start()

    def own_sent(self, q):
        for lane in (0, 1, 2):
            self.sent(lane, q, self.p.me)

    def forward(self, q):
        p = self.p
        self.arrived(1, q, p.x)
        self.pass_on(3, q, p.x, p.pair)

        @pl.when(lax.rem(q, 2) == 0)
        def _():
            self.pass_on(6, q, p.x, p.y)

        self.arrived(2, q, p.y)
        self.pass_on(4, q, p.y, p.pair)

        @pl.when(lax.rem(q, 2) == 1)
        def _():
            self.pass_on(6, q, p.y, p.x)

    def forward_diag(self, q):
        self.arrived(6, q, self.p.diag)
        self.pass_on(5, q, self.p.diag, self.p.pair)

    def finish(self, q):
        p = self.p
        for lane, owner in ((0, p.pair), (3, p.pair_x), (4, p.pair_y), (5, p.pair_diag)):
            self.arrived(lane, q, owner)
        for lane, owner in ((3, p.x), (4, p.y), (5, p.diag), (6, p.x)):
            self.sent(lane, q, owner)


def enter(me, tp):
    barrier = pltpu.get_barrier_semaphore()
    for o in range(1, 8):
        pl.semaphore_signal(barrier, inc=1, device_id={'dp': lax.rem(me + o, 8)}, device_id_type=MESH)
    for o in range(1, 4):
        pl.semaphore_signal(barrier, inc=1, device_id={'tp': lax.rem(tp + o, 4)}, device_id_type=MESH)
    pl.semaphore_wait(barrier, 10)


class Exchange:
    def __init__(self, axis, size, buf, send_sems, recv_sems):
        self.axis, self.size, self.buf, self.s, self.r = axis, size, buf, send_sems, recv_sems
        self.me = lax.axis_index(axis)

    def copy(self, o, src, slot):
        return pltpu.make_async_remote_copy(
            src_ref=src, dst_ref=self.buf.at[slot], send_sem=self.s.at[o], recv_sem=self.r.at[o],
            device_id={self.axis: lax.rem(self.me + o, self.size)}, device_id_type=MESH)

    def start(self, src):
        for o in range(1, self.size):
            self.copy(o, src, self.me).start()

    def wait(self, src):
        for o in range(1, self.size):
            self.copy(o, src, lax.rem(self.me + self.size - o, self.size)).wait_recv()
        for o in range(1, self.size):
            self.copy(o, src, self.me).wait_send()


def offsets(groups, lanes):
    return 8 * lax.broadcasted_iota(jnp.int32, (groups, 8, lanes), 0)


def own_tokens_kernel(z_ref, zf_ref, e_ref, info_ref, zall_ref, dzh_ref, info_out, lse_out, dz_ref, half_in,
                      logits, eslot, top, total, target, rows8, infobuf, stat, statbuf, lsend, lsebuf,
                      e_sem, half_s, half_r, zs, zr, info_s, info_r, stat_s, stat_r, lse_s, lse_r):
    plane = Plane()
    me, tp = plane.me, lax.axis_index('tp')
    enter(me, tp)

    def zregion(owner, q):
        return zall_ref.at[owner, pl.ds(pl.multiple_of(q * CHUNK, CHUNK), CHUNK), :]

    gather = Gather(plane, zregion, zs, zr)
    infos = Exchange('dp', 8, infobuf, info_s, info_r)
    infos.start(info_ref)
    for q in range(4):
        gather.send_own(q, zf_ref.at[pl.ds(q * CHUNK, CHUNK), :])
    infobuf[me] = info_ref[...]

    def fetch(j, slot):
        return pltpu.make_async_copy(
            e_ref.at[pl.ds(pl.multiple_of(j * BLOCK, BLOCK), BLOCK), :], eslot.at[slot], e_sem.at[slot])

    def fetch_rest(slot):
        return pltpu.make_async_copy(
            e_ref.at[pl.ds(FULL * BLOCK, REST), :], eslot.at[slot, pl.ds(0, REST), :], e_sem.at[slot])

    def blocks(body):
        fetch(0, 0).start()

        def step(j, _):
            slot = lax.rem(j, 2)
            fetch(j, slot).wait()

            @pl.when(j < FULL - 1)
            def _():
                fetch(j + 1, 1 - slot).start()

            @pl.when(j == FULL - 1)
            def _():
                eslot[1 - slot, pl.ds(272, RESTPAD - 272), :] = jnp.zeros((RESTPAD - 272, WIDTH), BF16)
                fetch_rest(1 - slot).start()

            body(pl.multiple_of(j * BLOCK, BLOCK), slot, BLOCK)
            return 0

        lax.fori_loop(0, FULL, step, 0)
        fetch_rest(FULL % 2).wait()
        body(FULL * BLOCK, FULL % 2, RESTPAD)

    sub = lax.broadcasted_iota(jnp.int32, (8, SEQ), 0)
    rows8[0] = jnp.broadcast_to(info_ref[2:3, :].astype(jnp.int32), (8, SEQ)) - sub
    top[...] = jnp.full((8, SEQ), -jnp.inf, F32)
    total[...] = jnp.zeros((8, SEQ), F32)
    target[...] = jnp.zeros((8, SEQ), F32)

    def forward_block(at, slot, n):
        e = eslot[slot, pl.ds(0, n), :]
        for t in range(4):
            cols = pl.ds(t * CHUNK, CHUNK)
            l = lax.dot_general(e, z_ref[cols, :], (((1,), (1,)), ((), ())), preferred_element_type=F32)
            if n != BLOCK:
                l = jnp.where(lax.broadcasted_iota(jnp.int32, (n, CHUNK), 0) < REST, l, -jnp.inf)
            logits[pl.ds(at, n), cols] = l
            l = l.reshape(n // 8, 8, CHUNK)
            old = top[:, cols]
            new = jnp.maximum(old, jnp.max(l, axis=0))
            top[:, cols] = new
            total[:, cols] = total[:, cols] * jnp.exp(old - new) + jnp.sum(jnp.exp(l - new[None]), axis=0)
            hit = offsets(n // 8, CHUNK) == (rows8[0, :, cols] - at)[None]
            target[:, cols] += jnp.sum(jnp.where(hit, l, 0.0), axis=0)

    blocks(forward_block)

    m1 = jnp.max(top[...], axis=0, keepdims=True)
    stat[0:1, :] = m1
    stat[1:2, :] = jnp.sum(total[...] * jnp.exp(top[...] - m1), axis=0, keepdims=True)
    stat[2:3, :] = jnp.sum(target[...], axis=0, keepdims=True)
    stats = Exchange('tp', 4, statbuf, stat_s, stat_r)
    stats.start(stat)
    statbuf[tp] = stat[...]
    infos.wait(info_ref)
    token_count = jnp.sum(infobuf[:, 1, :], keepdims=True)
    stats.wait(stat)
    m4 = jnp.max(statbuf[:, 0, :], axis=0, keepdims=True)
    s4 = jnp.sum(statbuf[:, 1, :] * jnp.exp(statbuf[:, 0, :] - m4), axis=0, keepdims=True)
    lse = m4 + jnp.log(s4)
    lsend[0:1, :] = lse
    lsend[1:2, :] = jnp.sum(statbuf[:, 2, :], axis=0, keepdims=True)
    lses = Exchange('dp', 8, lsebuf, lse_s, lse_r)
    lses.start(lsend)
    lsebuf[me] = lsend[...]
    top[...] = jnp.broadcast_to(lse, (8, SEQ))
    total[...] = jnp.broadcast_to(info_ref[1:2, :] / token_count, (8, SEQ))
    gather.forward(0)

    dz_ref[...] = jnp.zeros((SEQ, WIDTH), F32)

    def backward_block(at, slot, n):
        e = eslot[slot, pl.ds(0, n), :]
        for t in range(4):
            cols = pl.ds(t * CHUNK, CHUNK)
            l = logits[pl.ds(at, n), cols].reshape(n // 8, 8, CHUNK)
            p = jnp.exp(l - top[:, cols][None])
            hit = offsets(n // 8, CHUNK) == (rows8[0, :, cols] - at)[None]
            g = (jnp.where(hit, p - 1.0, p) * total[:, cols][None]).reshape(n, CHUNK).astype(BF16)
            dz_ref[cols, :] += lax.dot_general(g, e, (((0,), (0,)), ((), ())), preferred_element_type=F32)

    blocks(backward_block)

    mine = pl.multiple_of(lax.rem(tp, 2) * HALF, HALF)
    theirs = pl.multiple_of(HALF - lax.rem(tp, 2) * HALF, HALF)
    halves = pltpu.make_async_remote_copy(
        src_ref=dz_ref.at[pl.ds(theirs, HALF), :], dst_ref=half_in, send_sem=half_s, recv_sem=half_r,
        device_id={'tp': tp + 1 - 2 * lax.rem(tp, 2)}, device_id_type=MESH)
    halves.start()
    for q in range(1, 4):
        gather.forward(q)
    lses.wait(lsend)
    info_out[...] = infobuf[...]
    lse_out[...] = lsebuf[...]
    for q in range(4):
        gather.forward_diag(q)
    halves.wait()
    dzh_ref[...] = dz_ref[pl.ds(mine, HALF), :] + half_in[...]
    for q in range(4):
        gather.own_sent(q)
        gather.finish(q)


def own_tokens(z, zf, embed, info):
    return pl.pallas_call(
        own_tokens_kernel,
        name='own_tokens',
        out_shape=(
            jax.ShapeDtypeStruct((8, SEQ, WIDTH), F32),
            jax.ShapeDtypeStruct((HALF, WIDTH), F32),
            jax.ShapeDtypeStruct((8, 8, SEQ), F32),
            jax.ShapeDtypeStruct((8, 8, SEQ), F32),
        ),
        in_specs=[
            pl.BlockSpec(memory_space=pltpu.VMEM),
            pl.BlockSpec(memory_space=pl.ANY),
            pl.BlockSpec(memory_space=pl.ANY),
            pl.BlockSpec(memory_space=pltpu.VMEM),
        ],
        out_specs=(
            pl.BlockSpec(memory_space=pl.ANY),
            pl.BlockSpec(memory_space=pltpu.VMEM),
            pl.BlockSpec(memory_space=pltpu.VMEM),
            pl.BlockSpec(memory_space=pltpu.VMEM),
        ),
        scratch_shapes=[
            pltpu.VMEM((SEQ, WIDTH), F32),
            pltpu.VMEM((HALF, WIDTH), F32),
            pltpu.VMEM((FULL * BLOCK + RESTPAD, SEQ), F32),
            pltpu.VMEM((2, BLOCK, WIDTH), BF16),
            pltpu.VMEM((8, SEQ), F32),
            pltpu.VMEM((8, SEQ), F32),
            pltpu.VMEM((8, SEQ), F32),
            pltpu.VMEM((1, 8, SEQ), jnp.int32),
            pltpu.VMEM((8, 8, SEQ), F32),
            pltpu.VMEM((8, SEQ), F32),
            pltpu.VMEM((4, 8, SEQ), F32),
            pltpu.VMEM((8, SEQ), F32),
            pltpu.VMEM((8, 8, SEQ), F32),
            pltpu.SemaphoreType.DMA((2,)),
            pltpu.SemaphoreType.DMA,
            pltpu.SemaphoreType.DMA,
            pltpu.SemaphoreType.DMA((7, 4)),
            pltpu.SemaphoreType.DMA((7, 4)),
            pltpu.SemaphoreType.DMA((8,)),
            pltpu.SemaphoreType.DMA((8,)),
            pltpu.SemaphoreType.DMA((4,)),
            pltpu.SemaphoreType.DMA((4,)),
            pltpu.SemaphoreType.DMA((8,)),
            pltpu.SemaphoreType.DMA((8,)),
        ],
        compiler_params=pltpu.CompilerParams(collective_id=1, has_side_effects=True, vmem_limit_bytes=VMEM_LIMIT),
        cost_estimate=pl.CostEstimate(flops=4 * SEQ * ROWS * WIDTH, bytes_accessed=4 * ROWS * WIDTH, transcendentals=2 * SEQ * ROWS),
    )(z, zf, embed, info)


def all_tokens_kernel(z_ref, zall_ref, e_ref, info_ref, lse_ref, dz_ref, xhat_ref, inv_ref, gamma_ref, de_ref, dh_ref, sums_out,
                      far_in, dhh, zb, zslot, eslot, lbuf, stage, lse8, scale8, rows8, sums, sum4, sumbuf4, sumbuf8,
                      far_s, far_r, dh_sem, dh_s, dh_r, z_sem, e_sem, t_sem, l_sem, gs, gr, b_s, b_r, s4_s, s4_r, s8_s, s8_r):
    plane = Plane()
    me, tp = plane.me, lax.axis_index('tp')
    enter(me, tp)

    def fetch(at, n, slot):
        return pltpu.make_async_copy(e_ref.at[pl.ds(at, n), :], eslot.at[slot, pl.ds(0, n), :], e_sem.at[slot])

    def a_at(owner, q):
        return pl.multiple_of((owner * A_STEPS + q) * A_ROWS, A_ROWS)

    def b_at(core, b):
        return pl.multiple_of(A_TOTAL + (core * B_STEPS + b) * B_ROWS, 16)

    fetch(a_at(me, 0), A_ROWS, 0).start()
    tail = pltpu.make_async_copy(e_ref.at[pl.ds(TAIL_AT, TAIL), :], eslot.at[2, pl.ds(B_ROWS, TAIL), :], t_sem)
    tail.start()

    mine = pl.multiple_of(lax.rem(tp, 2) * HALF, HALF)
    far = pltpu.make_async_remote_copy(
        src_ref=dz_ref, dst_ref=far_in, send_sem=far_s, recv_sem=far_r,
        device_id={'tp': lax.rem(tp + 2, 4)}, device_id_type=MESH)
    far.start()

    def column_sums(i, carry):
        at = pl.multiple_of(i * 128, 128)
        dz = dz_ref[pl.ds(at, 128), :]
        dzx = dz * xhat_ref[pl.ds(mine + at, 128), :]
        return carry[0] + jnp.sum(dzx.reshape(16, 8, WIDTH), axis=0), carry[1] + jnp.sum(dz.reshape(16, 8, WIDTH), axis=0)

    zero = jnp.zeros((8, WIDTH), F32)
    dgamma, dbeta = lax.fori_loop(0, 4, column_sums, (zero, zero))
    sums[0:8, :] = dgamma
    sums[8:16, :] = dbeta
    over_tp = Exchange('tp', 4, sumbuf4, s4_s, s4_r)
    over_tp.start(sums)
    sumbuf4[tp] = sums[...]

    def fetch_z(n):
        owner = lax.rem(me + 1 + lax.div(n, 4), 8)
        q = pl.multiple_of(lax.rem(n, 4) * CHUNK, CHUNK)
        slot = lax.rem(n, 4)
        return owner, q, slot, pltpu.make_async_copy(zall_ref.at[owner, pl.ds(q, CHUNK), :], zslot.at[slot], z_sem.at[slot])

    for n in range(3):
        fetch_z(n)[3].start()
    zb[me] = z_ref[...]
    token_count = jnp.sum(info_ref[:, 1, :], keepdims=True)
    sub = lax.broadcasted_iota(jnp.int32, (8, SEQ), 0) + tp * ROWS
    for s in range(8):
        lse8[s] = jnp.broadcast_to(lse_ref[s, 0:1, :], (8, SEQ))
        scale8[s] = jnp.broadcast_to(info_ref[s, 1:2, :] / token_count, (8, SEQ))
        rows8[s] = jnp.broadcast_to(info_ref[s, 0:1, :].astype(jnp.int32), (8, SEQ)) - sub

    def convert(n, _):
        owner, q, slot, copy = fetch_z(n)
        copy.wait()

        @pl.when(n < 25)
        def _():
            fetch_z(n + 3)[3].start()

        zb[owner, pl.ds(q, CHUNK), :] = zslot[slot].astype(BF16)
        return 0

    lax.fori_loop(0, 28, convert, 0)

    def logits_of(slot, n, s):
        return lax.dot_general(eslot[slot, pl.ds(0, n), :], zb[s], (((1,), (1,)), ((), ())), preferred_element_type=F32)

    def grad_of(l, n, s, at, tail_at):
        l = l.reshape(n // 8, 8, SEQ)
        p = jnp.exp(l - lse8[s][None])
        row = offsets(n // 8, SEQ) + at
        if tail_at is not None:
            row = jnp.where(offsets(n // 8, SEQ) < B_ROWS, row, row + (tail_at - B_ROWS - at))
        g = jnp.where(row == rows8[s][None], p - 1.0, p) * scale8[s][None]
        return g.reshape(n, SEQ).astype(BF16)

    def compute(slot, out, n, at, tail_at=None):
        lbuf[0, pl.ds(0, n), :] = logits_of(slot, n, 0)
        stage[out, pl.ds(0, n), :] = jnp.zeros((n, WIDTH), F32)

        def one(s, k, last):
            if not last:
                lbuf[1 - k, pl.ds(0, n), :] = logits_of(slot, n, s + 1)
            g = grad_of(lbuf[k, pl.ds(0, n), :], n, s, at, tail_at)
            stage[out, pl.ds(0, n), :] += jnp.dot(g, zb[s], preferred_element_type=F32)

        def pairs(i, _):
            one(2 * i, 0, False)
            one(2 * i + 1, 1, False)
            return 0

        lax.fori_loop(0, 3, pairs, 0)
        one(6, 0, False)
        one(7, 1, True)

    def region(owner, q):
        return de_ref.at[pl.ds(a_at(owner, q), A_ROWS), :]

    gather = Gather(plane, region, gs, gr)

    def keep(out, n, at):
        return pltpu.make_async_copy(stage.at[out, pl.ds(0, n), :], de_ref.at[pl.ds(at, n), :], l_sem.at[out])

    def a_step(q, _):
        slot = lax.rem(q, 2)
        fetch(a_at(me, q), A_ROWS, slot).wait()

        @pl.when(q < A_STEPS - 1)
        def _():
            fetch(a_at(me, q + 1), A_ROWS, 1 - slot).start()

        @pl.when(q == A_STEPS - 1)
        def _():
            fetch(b_at(plane.core, 0), B_ROWS, 1 - slot).start()

        compute(slot, 2 + q, A_ROWS, a_at(me, q))
        keep(2 + q, A_ROWS, a_at(me, q)).start()
        gather.send_own(q, stage.at[2 + q, pl.ds(0, A_ROWS), :])
        return 0

    lax.fori_loop(0, A_STEPS, a_step, 0)

    over_tp.wait(sums)
    sum4[...] = sumbuf4[0] + sumbuf4[1] + sumbuf4[2] + sumbuf4[3]
    over_dp = Exchange('dp', 8, sumbuf8, s8_s, s8_r)
    over_dp.start(sum4)
    sumbuf8[me] = sum4[...]

    def b_copy(b, out, core):
        at = b_at(core, b)
        return pltpu.make_async_remote_copy(
            src_ref=stage.at[out, pl.ds(0, B_ROWS), :], dst_ref=de_ref.at[pl.ds(at, B_ROWS), :],
            send_sem=b_s.at[b], recv_sem=b_r.at[b], device_id={'dp': plane.pair}, device_id_type=MESH)

    def b_free(b, slot):
        @pl.when(b >= 2)
        def _():
            keep(slot, B_ROWS, b_at(plane.core, b - 2)).wait()
            b_copy(b - 2, slot, plane.core).wait_send()

    home = pltpu.make_async_copy(dhh, dh_ref.at[pl.ds(mine, HALF), :], dh_sem)
    dh_pair = pltpu.make_async_remote_copy(
        src_ref=dhh, dst_ref=dh_ref.at[pl.ds(mine, HALF), :], send_sem=dh_s, recv_sem=dh_r,
        device_id={'tp': tp + 1 - 2 * lax.rem(tp, 2)}, device_id_type=MESH)
    dh_from_pair = pltpu.make_async_remote_copy(
        src_ref=dhh, dst_ref=dh_ref.at[pl.ds(pl.multiple_of(HALF - mine, HALF), HALF), :], send_sem=dh_s, recv_sem=dh_r,
        device_id={'tp': tp + 1 - 2 * lax.rem(tp, 2)}, device_id_type=MESH)

    def half_grad():
        far.wait()

        def part(i, _):
            at = pl.multiple_of(i * 64, 64)
            xh = xhat_ref[pl.ds(mine + at, 64), :]
            g = (dz_ref[pl.ds(at, 64), :] + far_in[pl.ds(at, 64), :]) * gamma_ref[...]
            g = g - jnp.mean(g, axis=-1, keepdims=True) - xh * jnp.mean(g * xh, axis=-1, keepdims=True)
            dhh[pl.ds(at, 64), :] = g * inv_ref[pl.ds(mine + at, 64), :]
            return 0

        lax.fori_loop(0, HALF // 64, part, 0)
        home.start()
        dh_pair.start()

    def b_step(b, _):
        slot = lax.rem(b, 2)
        at = b_at(plane.core, b)
        fetch(at, B_ROWS, slot).wait()

        @pl.when(b < B_STEPS - 2)
        def _():
            fetch(b_at(plane.core, b + 1), B_ROWS, 1 - slot).start()

        @pl.when(b == B_STEPS - 2)
        def _():
            fetch(b_at(plane.core, B_STEPS - 1), B_ROWS, 2).start()

        @pl.when(lax.rem(b, 2) == 0)
        def _():
            gather.forward(lax.div(b, 2))

        @pl.when(b == 5)
        def _():
            half_grad()

        b_free(b, slot)
        compute(slot, slot, B_ROWS, at)
        keep(slot, B_ROWS, at).start()
        b_copy(b, slot, plane.core).start()
        return 0

    lax.fori_loop(0, B_STEPS - 1, b_step, 0)

    b, slot = B_STEPS - 1, (B_STEPS - 1) % 2
    at = b_at(plane.core, b)
    fetch(at, B_ROWS, 2).wait()
    tail.wait()
    gather.forward_diag(0)
    gather.forward_diag(1)
    b_free(b, slot)
    compute(2, slot, R_MAX, at, TAIL_AT)
    keep(slot, B_ROWS, at).start()
    b_copy(b, slot, plane.core).start()
    keep_tail = pltpu.make_async_copy(stage.at[slot, pl.ds(B_ROWS, TAIL), :], de_ref.at[pl.ds(TAIL_AT, TAIL), :], t_sem)
    keep_tail.start()

    over_dp.wait(sum4)
    sums_out[...] = jnp.sum(sumbuf8[...], axis=0)
    for q in range(2, A_STEPS):
        gather.forward_diag(q)
    keep(1 - slot, B_ROWS, b_at(plane.core, b - 1)).wait()
    b_copy(b - 1, 1 - slot, plane.core).wait_send()
    keep(slot, B_ROWS, at).wait()
    keep_tail.wait()
    b_copy(b, slot, plane.core).wait_send()
    for k in range(B_STEPS):
        b_copy(k, 0, 1 - plane.core).wait_recv()
    home.wait()
    dh_pair.wait_send()
    dh_from_pair.wait_recv()
    for q in range(A_STEPS):
        keep(2 + q, A_ROWS, a_at(me, q)).wait()
        gather.own_sent(q)
        gather.finish(q)


def all_tokens(z, zall, embed, info, lse, dz, xhat, inv_std, gamma):
    return pl.pallas_call(
        all_tokens_kernel,
        name='all_tokens',
        out_shape=(
            jax.ShapeDtypeStruct((ROWS, WIDTH), F32),
            jax.ShapeDtypeStruct((SEQ, WIDTH), F32),
            jax.ShapeDtypeStruct((16, WIDTH), F32),
        ),
        in_specs=[
            pl.BlockSpec(memory_space=pltpu.VMEM),
            pl.BlockSpec(memory_space=pl.ANY),
            pl.BlockSpec(memory_space=pl.ANY),
            pl.BlockSpec(memory_space=pltpu.VMEM),
            pl.BlockSpec(memory_space=pltpu.VMEM),
            pl.BlockSpec(memory_space=pltpu.VMEM),
            pl.BlockSpec(memory_space=pltpu.VMEM),
            pl.BlockSpec(memory_space=pltpu.VMEM),
            pl.BlockSpec(memory_space=pltpu.VMEM),
        ],
        out_specs=(
            pl.BlockSpec(memory_space=pl.ANY),
            pl.BlockSpec(memory_space=pl.ANY),
            pl.BlockSpec(memory_space=pltpu.VMEM),
        ),
        scratch_shapes=[
            pltpu.VMEM((HALF, WIDTH), F32),
            pltpu.VMEM((HALF, WIDTH), F32),
            pltpu.VMEM((8, SEQ, WIDTH), BF16),
            pltpu.VMEM((4, CHUNK, WIDTH), F32),
            pltpu.VMEM((3, R_MAX + 8, WIDTH), BF16),
            pltpu.VMEM((2, R_MAX, SEQ), F32),
            pltpu.VMEM((2 + A_STEPS, R_MAX, WIDTH), F32),
            pltpu.VMEM((8, 8, SEQ), F32),
            pltpu.VMEM((8, 8, SEQ), F32),
            pltpu.VMEM((8, 8, SEQ), jnp.int32),
            pltpu.VMEM((16, WIDTH), F32),
            pltpu.VMEM((16, WIDTH), F32),
            pltpu.VMEM((4, 16, WIDTH), F32),
            pltpu.VMEM((8, 16, WIDTH), F32),
            pltpu.SemaphoreType.DMA,
            pltpu.SemaphoreType.DMA,
            pltpu.SemaphoreType.DMA,
            pltpu.SemaphoreType.DMA,
            pltpu.SemaphoreType.DMA,
            pltpu.SemaphoreType.DMA((4,)),
            pltpu.SemaphoreType.DMA((3,)),
            pltpu.SemaphoreType.DMA,
            pltpu.SemaphoreType.DMA((2 + A_STEPS,)),
            pltpu.SemaphoreType.DMA((7, A_STEPS)),
            pltpu.SemaphoreType.DMA((7, A_STEPS)),
            pltpu.SemaphoreType.DMA((B_STEPS,)),
            pltpu.SemaphoreType.DMA((B_STEPS,)),
            pltpu.SemaphoreType.DMA((4,)),
            pltpu.SemaphoreType.DMA((4,)),
            pltpu.SemaphoreType.DMA((8,)),
            pltpu.SemaphoreType.DMA((8,)),
        ],
        compiler_params=pltpu.CompilerParams(collective_id=2, has_side_effects=True, vmem_limit_bytes=60_000_000),
        cost_estimate=pl.CostEstimate(flops=32 * SEQ * 3200 * WIDTH, bytes_accessed=8 * ROWS * WIDTH, transcendentals=8 * SEQ * 3200),
    )(z, zall, embed, info, lse, dz, xhat, inv_std, gamma)


def solution(mesh):
    def local_step(hidden, ln_gamma, ln_beta, embed_shard, labels, loss_mask):
        shard_start = lax.axis_index('tp') * ROWS
        x_hat, inv_std, normed = layer_norm_fwd(hidden[0], ln_gamma, ln_beta)
        z = normed.astype(BF16)
        here = labels - shard_start
        here = jnp.where((here >= 0) & (here < ROWS), here, -1)
        info = jnp.concatenate([labels.astype(F32), loss_mask.astype(F32), here.astype(F32), jnp.zeros((5, SEQ), F32)], axis=0)
        zall, dz_half, info_all, lse_all = own_tokens(z, z.astype(F32), embed_shard, info)
        d_embed, d_rows, sums = all_tokens(z, zall, embed_shard, info_all, lse_all, dz_half, x_hat, inv_std, ln_gamma[None])
        mask = info_all[:, 1, :]
        mean_loss = jnp.sum(mask * (lse_all[:, 0, :] - lse_all[:, 1, :])) / jnp.sum(mask)
        d_gamma = jnp.sum(sums[:8], axis=0)
        d_beta = jnp.sum(sums[8:], axis=0)
        d_hidden = d_rows.astype(BF16)[None]
        return mean_loss, d_hidden, d_embed, d_gamma, d_beta

    return jax.shard_map(local_step, mesh=mesh, in_specs=(P('dp', None, None), P(None), P(None), P('tp', None), P('dp', None), P('dp', None)), out_specs=(P(), P('dp', None, None), P('tp', None), P(None), P(None)), check_vma=False)
```

time: 774 us -> 327 us (0.42)
  waiting for transfers between devices: 518 us -> 0 us
  Pallas kernels: 0 us -> 277 us
  matrix products: 96.7 us -> 0 us
  blocking collectives: 51.2 us -> 0 us
  other arithmetic: 62.2 us -> 14.6 us
  between operations: 16.6 us -> 3.21 us
    psum x2 -> x0, waiting for transfers between devices: 518 us -> none  [the longest x1 433 us: local_step(): lax.psum(jnp.einsum('bsv,bsd->vd', grad_logits, normed, preferred_element...]
    pallas_call x0 -> x2, Pallas kernels: none -> 277 us  [the longest x1 157 us: all_tokens(): pl.pallas_call(all_tokens_kernel, name='all_tokens', out_shape=(jax.Shape...]
    dot_general x3 -> x0, matrix products: 96.7 us -> none  [the longest x1 38.1 us: local_step(): jnp.einsum('bsd,vd->bsv', normed, embed_shard, preferred_element_type=jnp...]
    psum x3 -> x0, blocking collectives: 39.2 us -> none  [the longest x1 15.8 us: local_step(): token_count = lax.psum(jnp.sum(mask_float), 'dp')]
    convert_element_type x2 -> x3, other arithmetic: 29.8 us -> 4.59 us  [the longest x1 3.89 us: local_step(): z.astype(F32)]
    reduce_sum x4 -> x2, other arithmetic: 27.3 us -> 2.41 us  [the longest x1 1.8 us: local_step(): jnp.sum(mask)]
    pmax x1 -> x0, blocking collectives: 11.9 us -> none  [local_step(): row_max = lax.pmax(jnp.max(logits, axis=-1, keepdims=True), 'tp')]
  transfers between devices with their start and end apart: 2 -> 0, of which waited for: 2 -> 0; matrix products, arithmetic and copies ran while one was open for 5% -> 0% of each run, Pallas kernels for 0% -> 0%
where the time goes in v1:
time: 327 us; the launch traced here: 325 us
  Pallas kernels  277 us (85%)
  local copies, waits for them, and re-layouts  29.8 us (9%)
  other arithmetic  14.6 us (4%)
    pallas_call x1, Pallas kernels, all_tokens(): pl.pallas_call(all_tokens_kernel, name='all_tokens', out_shape=(jax.Shape...  157 us
    pallas_call x1, Pallas kernels, own_tokens(): pl.pallas_call(own_tokens_kernel, name='own_tokens', out_shape=(jax.Shape...  120 us
    unnamed x11, local copies, waits for them, and re-layouts  27.3 us

profile of v1, /device:TPU:0, one launch (start us, length us, event | category | flops | bytes accessed | tf_op | source)
XLA Modules:
  0.0 324.9 jit_solution(14097513796451509406)
XLA Ops:
  0.6 0.0 copy-start
  0.6 0.0 copy-start.2
  0.7 0.0 copy-start.4
  0.7 0.0 copy-start.3
  0.7 0.1 pad.3.clone
  0.8 1.4 broadcast_in_dim.19.gamma_ref
  2.1 0.7 convert_element_type.29
  2.8 1.7 convert_reduce_fusion
  4.5 2.0 fusion.3
  6.5 0.0 copy-done.4
  6.6 0.7 maximum_maximum_fusion.info_ref
  7.3 1.0 copy.11.inv_ref
  8.3 0.0 copy-done
  8.3 0.0 copy-done.2
  8.3 0.0 copy-done.3
  8.3 3.9 %fusion.5 = (f32[1024,768]{1,0:T(8,128)}, bf16[1024,768]{1,0:T(8,128)(2,1)}, f32[1024,768]{1,0:T(8,128)}) fusion(f32[768]{0:T(1024)S(1)} %copy-done.3, f32[768]{0:T(1024)S(1)} %copy-done.2, f32[1024]{0:T(1024)S(1)} %add_rsqrt_fusion, f32[1024]{0:T(1024)S(1)} %broadcast_multiply_fusion, bf16[1,1024,768]{2,1,0:T(8,128)(2,1)S(1)} %copy-done), kind=kLoop, calls=%fused_computation.17 | loop fusion | flops 5505024 | bytes 9451520 | tf_op jit(solution)/shard_map/convert_element_type | solution.py:622
  12.2 120.5 %own_tokens.1 = (f32[8,1024,768]{2,1,0:T(8,128)}, f32[512,768]{1,0:T(8,128)}, f32[8,8,1024]{2,1,0:T(8,128)}, f32[8,8,1024]{2,1,0:T(8,128)}) custom-call(bf16[1024,768]{1,0:T(8,128)(2,1)} %get-tuple-element.24.z_ref, f32[1024,768]{1,0:T(8,128)} %get-tuple-element.23.zf_ref, bf16[12568,768]{1,0:T(8,128)(2,1)} %e_ref.3, f32[8,1024]{1,0:T(8,128)} %maximum_maximum_fusion.info_ref), custom_call_target="tpu_custom_call" | custom-call | flops 39535509504 | bytes 38608896 | tf_op jit(solution)/shard_map/own_tokens/pallas_call | solution.py:269
  132.7 1.8 slice_reduce_fusion.2
  135.8 156.8 %all_tokens.1 = (f32[12568,768]{1,0:T(8,128)}, f32[1024,768]{1,0:T(8,128)}, f32[16,768]{1,0:T(8,128)}) custom-call(bf16[1024,768]{1,0:T(8,128)(2,1)} %get-tuple-element.24.z_ref, f32[8,1024,768]{2,1,0:T(8,128)} %get-tuple-element.14.zall_ref, bf16[12568,768]{1,0:T(8,128)(2,1)} %e_ref.3, f32[8,8,1024]{2,1,0:T(8,128)} %get-tuple-element.12.info_ref, ...), custom_call_target="tpu_custom_call" | custom-call | flops 80530636800 | bytes 77217792 | tf_op jit(solution)/shard_map/all_tokens/pallas_call | solution.py:552
  292.6 0.0 copy-start.1
  292.7 3.2 convert_bitcast_fusion.1
  295.9 0.0 copy-done.1
  295.9 0.6 slice_reduce_fusion
  296.5 27.3 %copy.13 = f32[12568,768]{1,0:T(8,128)} copy(f32[12568,768]{1,0:T(8,128)} %get-tuple-element.35) | data formatting | bytes 77217792
  (4 shorter events, 0.0 us)
Async XLA Ops:
  0.6 7.6 %copy-start = (bf16[1,1024,768]{2,1,0:T(8,128)(2,1)S(1)}, bf16[1,1024,768]{2,1,0:T(8,128)(2,1)}, u32[]{:S(2)}) copy-start(bf16[1,1024,768]{2,1,0:T(8,128)(2,1)} %param.6) | copy-start | bytes 4718596
  0.6 7.6 %copy-start.2 = (f32[768]{0:T(1024)S(1)}, f32[768]{0:T(1024)}, u32[]{:S(2)}) copy-start(f32[768]{0:T(1024)} %param.7) | copy-start | bytes 9220
  0.7 5.9 %copy-start.4 = (s32[1,1024]{1,0:T(1,128)S(1)}, s32[1,1024]{1,0:T(1,128)}, u32[]{:S(2)}) copy-start(s32[1,1024]{1,0:T(1,128)} %param.10) | copy-start | bytes 12292
  0.7 7.6 %copy-start.3 = (f32[768]{0:T(1024)S(1)}, f32[768]{0:T(1024)}, u32[]{:S(2)}) copy-start(f32[768]{0:T(1024)} %param.8) | copy-start | bytes 9220
  292.6 3.2 copy-start.1

commit v2 on v1

--- a/solution.py
+++ b/solution.py
@@ -15,9 +15,10 @@
 REST = ROWS - FULL * BLOCK
 RESTPAD = 384
 CHUNK = 256
+Z_SLOTS = 6
 HALF = 512
-A_ROWS, A_STEPS = 256, 4
-B_ROWS, B_STEPS = 272, 8
+A_ROWS, A_STEPS = 240, 4
+B_ROWS, B_STEPS = 608, 4
 A_TOTAL = 8 * A_ROWS * A_STEPS
 TAIL = ROWS - A_TOTAL - 2 * B_ROWS * B_STEPS
 TAIL_AT = ROWS - TAIL
@@ -80,14 +81,14 @@
         self.arrived(1, q, p.x)
         self.pass_on(3, q, p.x, p.pair)
 
-        @pl.when(lax.rem(q, 2) == 0)
+        @pl.when(lax.rem(q + p.core, 2) == 0)
         def _():
             self.pass_on(6, q, p.x, p.y)
 
         self.arrived(2, q, p.y)
         self.pass_on(4, q, p.y, p.pair)
 
-        @pl.when(lax.rem(q, 2) == 1)
+        @pl.when(lax.rem(q + p.core, 2) == 1)
         def _():
             self.pass_on(6, q, p.y, p.x)
 
@@ -112,6 +113,14 @@
     pl.semaphore_wait(barrier, 10)
 
 
+class Quarters:
+    def __init__(self, tp):
+        self.partner = (tp + 1 - 2 * lax.rem(tp, 2), 3 - tp)
+        first, second = lax.rem(lax.div(tp + 1, 2), 2) * CHUNK, lax.div(tp, 2) * CHUNK
+        self.mine = (pl.multiple_of(first, CHUNK), pl.multiple_of(HALF + second, CHUNK))
+        self.theirs = (pl.multiple_of(CHUNK - first, CHUNK), pl.multiple_of(HALF + CHUNK - second, CHUNK))
+
+
 class Exchange:
     def __init__(self, axis, size, buf, send_sems, recv_sems):
         self.axis, self.size, self.buf, self.s, self.r = axis, size, buf, send_sems, recv_sems
@@ -137,21 +146,31 @@
     return 8 * lax.broadcasted_iota(jnp.int32, (groups, 8, lanes), 0)
 
 
-def own_tokens_kernel(z_ref, zf_ref, e_ref, info_ref, zall_ref, dzh_ref, info_out, lse_out, dz_ref, half_in,
+def own_tokens_kernel(z_ref, zf_ref, e_ref, info_ref, zall_ref, dz_ref, info_out, lse_out,
                       logits, eslot, top, total, target, rows8, infobuf, stat, statbuf, lsend, lsebuf,
                       e_sem, half_s, half_r, zs, zr, info_s, info_r, stat_s, stat_r, lse_s, lse_r):
     plane = Plane()
     me, tp = plane.me, lax.axis_index('tp')
     enter(me, tp)
 
+    odd = lax.rem(tp, 2)
+    starts = tuple(pl.multiple_of(s, CHUNK) for s in ((2 + odd) * CHUNK, 0, CHUNK, (3 - odd) * CHUNK))
+
     def zregion(owner, q):
-        return zall_ref.at[owner, pl.ds(pl.multiple_of(q * CHUNK, CHUNK), CHUNK), :]
+        return zall_ref.at[owner, pl.ds(starts[q], CHUNK), :]
+
+    def across(i, owner, q):
+        part = zregion(owner, q)
+        return pltpu.make_async_remote_copy(
+            src_ref=part, dst_ref=part, send_sem=half_s.at[i], recv_sem=half_r.at[i],
+            device_id={'tp': tp + 1 - 2 * odd}, device_id_type=MESH)
 
     gather = Gather(plane, zregion, zs, zr)
     infos = Exchange('dp', 8, infobuf, info_s, info_r)
     infos.start(info_ref)
-    for q in range(4):
-        gather.send_own(q, zf_ref.at[pl.ds(q * CHUNK, CHUNK), :])
+    own = tuple(zf_ref.at[pl.ds(s, CHUNK), :] for s in starts)
+    gather.send_own(0, own[0])
+    gather.copy(0, 3, own[3], zregion(me, 3), plane.pair).start()
     infobuf[me] = info_ref[...]
 
     def fetch(j, slot):
@@ -162,7 +181,7 @@
         return pltpu.make_async_copy(
             e_ref.at[pl.ds(FULL * BLOCK, REST), :], eslot.at[slot, pl.ds(0, REST), :], e_sem.at[slot])
 
-    def blocks(body):
+    def blocks(body, hooks):
         fetch(0, 0).start()
 
         def step(j, _):
@@ -178,6 +197,8 @@
                 eslot[1 - slot, pl.ds(272, RESTPAD - 272), :] = jnp.zeros((RESTPAD - 272, WIDTH), BF16)
                 fetch_rest(1 - slot).start()
 
+            for at, hook in hooks:
+                pl.when(j == at)(hook)
             body(pl.multiple_of(j * BLOCK, BLOCK), slot, BLOCK)
             return 0
 
@@ -207,7 +228,13 @@
             hit = offsets(n // 8, CHUNK) == (rows8[0, :, cols] - at)[None]
             target[:, cols] += jnp.sum(jnp.where(hit, l, 0.0), axis=0)
 
-    blocks(forward_block)
+    def first_chunk():
+        gather.forward(0)
+        across(0, plane.x, 0).start()
+        gather.send_own(1, own[1])
+        gather.send_own(2, own[2])
+
+    blocks(forward_block, ((12, first_chunk),))
 
     m1 = jnp.max(top[...], axis=0, keepdims=True)
     stat[0:1, :] = m1
@@ -229,7 +256,9 @@
     lsebuf[me] = lsend[...]
     top[...] = jnp.broadcast_to(lse, (8, SEQ))
     total[...] = jnp.broadcast_to(info_ref[1:2, :] / token_count, (8, SEQ))
-    gather.forward(0)
+    across(1, plane.y, 0).start()
+    gather.forward_diag(0)
+    across(2, plane.diag, 0).start()
 
     dz_ref[...] = jnp.zeros((SEQ, WIDTH), F32)
 
@@ -243,26 +272,25 @@
             g = (jnp.where(hit, p - 1.0, p) * total[:, cols][None]).reshape(n, CHUNK).astype(BF16)
             dz_ref[cols, :] += lax.dot_general(g, e, (((0,), (0,)), ((), ())), preferred_element_type=F32)
 
-    blocks(backward_block)
-
-    mine = pl.multiple_of(lax.rem(tp, 2) * HALF, HALF)
-    theirs = pl.multiple_of(HALF - lax.rem(tp, 2) * HALF, HALF)
-    halves = pltpu.make_async_remote_copy(
-        src_ref=dz_ref.at[pl.ds(theirs, HALF), :], dst_ref=half_in, send_sem=half_s, recv_sem=half_r,
-        device_id={'tp': tp + 1 - 2 * lax.rem(tp, 2)}, device_id_type=MESH)
-    halves.start()
-    for q in range(1, 4):
-        gather.forward(q)
+    blocks(backward_block, ((8, lambda: gather.forward(1)), (18, lambda: gather.forward(2))))
+
+    for i, (lane, owner) in enumerate(((3, plane.x), (4, plane.y), (5, plane.diag))):
+        across(i, owner, 3).wait_recv()
+        gather.pass_on(lane, 3, owner, plane.pair)
     lses.wait(lsend)
     info_out[...] = infobuf[...]
     lse_out[...] = lsebuf[...]
-    for q in range(4):
+    for q in (1, 2):
         gather.forward_diag(q)
-    halves.wait()
-    dzh_ref[...] = dz_ref[pl.ds(mine, HALF), :] + half_in[...]
-    for q in range(4):
+    for q in range(3):
         gather.own_sent(q)
         gather.finish(q)
+    gather.sent(0, 3, me)
+    for lane, owner in ((0, plane.pair), (3, plane.pair_x), (4, plane.pair_y), (5, plane.pair_diag)):
+        gather.arrived(lane, 3, owner)
+    for i, (lane, owner) in enumerate(((3, plane.x), (4, plane.y), (5, plane.diag))):
+        gather.sent(lane, 3, owner)
+        across(i, owner, 0).wait_send()
 
 
 def own_tokens(z, zf, embed, info):
@@ -271,7 +299,7 @@
         name='own_tokens',
         out_shape=(
             jax.ShapeDtypeStruct((8, SEQ, WIDTH), F32),
-            jax.ShapeDtypeStruct((HALF, WIDTH), F32),
+            jax.ShapeDtypeStruct((SEQ, WIDTH), F32),
             jax.ShapeDtypeStruct((8, 8, SEQ), F32),
             jax.ShapeDtypeStruct((8, 8, SEQ), F32),
         ),
@@ -288,8 +316,6 @@
             pl.BlockSpec(memory_space=pltpu.VMEM),
         ),
         scratch_shapes=[
-            pltpu.VMEM((SEQ, WIDTH), F32),
-            pltpu.VMEM((HALF, WIDTH), F32),
             pltpu.VMEM((FULL * BLOCK + RESTPAD, SEQ), F32),
             pltpu.VMEM((2, BLOCK, WIDTH), BF16),
             pltpu.VMEM((8, SEQ), F32),
@@ -302,8 +328,8 @@
             pltpu.VMEM((8, SEQ), F32),
             pltpu.VMEM((8, 8, SEQ), F32),
             pltpu.SemaphoreType.DMA((2,)),
-            pltpu.SemaphoreType.DMA,
-            pltpu.SemaphoreType.DMA,
+            pltpu.SemaphoreType.DMA((3,)),
+            pltpu.SemaphoreType.DMA((3,)),
             pltpu.SemaphoreType.DMA((7, 4)),
             pltpu.SemaphoreType.DMA((7, 4)),
             pltpu.SemaphoreType.DMA((8,)),
@@ -318,9 +344,9 @@
     )(z, zf, embed, info)
 
 
-def all_tokens_kernel(z_ref, zall_ref, e_ref, info_ref, lse_ref, dz_ref, xhat_ref, inv_ref, gamma_ref, de_ref, dh_ref, sums_out,
-                      far_in, dhh, zb, zslot, eslot, lbuf, stage, lse8, scale8, rows8, sums, sum4, sumbuf4, sumbuf8,
-                      far_s, far_r, dh_sem, dh_s, dh_r, z_sem, e_sem, t_sem, l_sem, gs, gr, b_s, b_r, s4_s, s4_r, s8_s, s8_r):
+def all_tokens_kernel(z_ref, zall_ref, e_ref, info_ref, lse_ref, dzp_ref, xhat_ref, inv_ref, gamma_ref, de_ref, dh_ref, sums_out,
+                      half_in, dzh, far_in, dhh, zb, zslot, eslot, lbuf, stage_a, stage_b, lse8, scale8, rows8, sums, sum4, sumbuf4, sumbuf8,
+                      half_s, half_r, far_s, far_r, dh_sem, dh_s, dh_r, z_sem, e_sem, t_sem, l_sem, gs, gr, b_s, b_r, s4_s, s4_r, s8_s, s8_r):
     plane = Plane()
     me, tp = plane.me, lax.axis_index('tp')
     enter(me, tp)
@@ -329,7 +355,7 @@
         return pltpu.make_async_copy(e_ref.at[pl.ds(at, n), :], eslot.at[slot, pl.ds(0, n), :], e_sem.at[slot])
 
     def a_at(owner, q):
-        return pl.multiple_of((owner * A_STEPS + q) * A_ROWS, A_ROWS)
+        return pl.multiple_of((owner * A_STEPS + q) * A_ROWS, 16)
 
     def b_at(core, b):
         return pl.multiple_of(A_TOTAL + (core * B_STEPS + b) * B_ROWS, 16)
@@ -338,33 +364,25 @@
     tail = pltpu.make_async_copy(e_ref.at[pl.ds(TAIL_AT, TAIL), :], eslot.at[2, pl.ds(B_ROWS, TAIL), :], t_sem)
     tail.start()
 
-    mine = pl.multiple_of(lax.rem(tp, 2) * HALF, HALF)
-    far = pltpu.make_async_remote_copy(
-        src_ref=dz_ref, dst_ref=far_in, send_sem=far_s, recv_sem=far_r,
-        device_id={'tp': lax.rem(tp + 2, 4)}, device_id_type=MESH)
-    far.start()
-
-    def column_sums(i, carry):
-        at = pl.multiple_of(i * 128, 128)
-        dz = dz_ref[pl.ds(at, 128), :]
-        dzx = dz * xhat_ref[pl.ds(mine + at, 128), :]
-        return carry[0] + jnp.sum(dzx.reshape(16, 8, WIDTH), axis=0), carry[1] + jnp.sum(dz.reshape(16, 8, WIDTH), axis=0)
-
-    zero = jnp.zeros((8, WIDTH), F32)
-    dgamma, dbeta = lax.fori_loop(0, 4, column_sums, (zero, zero))
-    sums[0:8, :] = dgamma
-    sums[8:16, :] = dbeta
-    over_tp = Exchange('tp', 4, sumbuf4, s4_s, s4_r)
-    over_tp.start(sums)
-    sumbuf4[tp] = sums[...]
+    quarters = Quarters(tp)
+
+    def swap_with(k, partner, src, dst, send_sem, recv_sem):
+        return pltpu.make_async_remote_copy(
+            src_ref=src, dst_ref=dst.at[k], send_sem=send_sem.at[k], recv_sem=recv_sem.at[k],
+            device_id={'tp': partner}, device_id_type=MESH)
+
+    nears = [swap_with(k, quarters.partner[k], dzp_ref.at[pl.ds(quarters.theirs[k], CHUNK), :], half_in, half_s, half_r) for k in range(2)]
+    fars = [swap_with(k, quarters.partner[1 - k], dzh.at[k], far_in, far_s, far_r) for k in range(2)]
+    for near in nears:
+        near.start()
 
     def fetch_z(n):
         owner = lax.rem(me + 1 + lax.div(n, 4), 8)
         q = pl.multiple_of(lax.rem(n, 4) * CHUNK, CHUNK)
-        slot = lax.rem(n, 4)
+        slot = lax.rem(n, Z_SLOTS)
         return owner, q, slot, pltpu.make_async_copy(zall_ref.at[owner, pl.ds(q, CHUNK), :], zslot.at[slot], z_sem.at[slot])
 
-    for n in range(3):
+    for n in range(Z_SLOTS - 1):
         fetch_z(n)[3].start()
     zb[me] = z_ref[...]
     token_count = jnp.sum(info_ref[:, 1, :], keepdims=True)
@@ -378,14 +396,12 @@
         owner, q, slot, copy = fetch_z(n)
         copy.wait()
 
-        @pl.when(n < 25)
-        def _():
-            fetch_z(n + 3)[3].start()
+        @pl.when(n < 29 - Z_SLOTS)
+        def _():
+            fetch_z(n + Z_SLOTS - 1)[3].start()
 
         zb[owner, pl.ds(q, CHUNK), :] = zslot[slot].astype(BF16)
         return 0
-
-    lax.fori_loop(0, 28, convert, 0)
 
     def logits_of(slot, n, s):
         return lax.dot_general(eslot[slot, pl.ds(0, n), :], zb[s], (((1,), (1,)), ((), ())), preferred_element_type=F32)
@@ -399,15 +415,18 @@
         g = jnp.where(row == rows8[s][None], p - 1.0, p) * scale8[s][None]
         return g.reshape(n, SEQ).astype(BF16)
 
-    def compute(slot, out, n, at, tail_at=None):
-        lbuf[0, pl.ds(0, n), :] = logits_of(slot, n, 0)
-        stage[out, pl.ds(0, n), :] = jnp.zeros((n, WIDTH), F32)
-
-        def one(s, k, last):
+    def compute(slot, out, n, at, tail_at=None, arriving=False):
+        lbuf[0, pl.ds(0, n), :] = logits_of(slot, n, me)
+        out[...] = jnp.zeros((n, WIDTH), F32)
+
+        def one(i, k, last):
+            s = lax.rem(me + i, 8)
             if not last:
-                lbuf[1 - k, pl.ds(0, n), :] = logits_of(slot, n, s + 1)
+                if arriving:
+                    lax.fori_loop(4 * i, 4 * i + 4, convert, 0)
+                lbuf[1 - k, pl.ds(0, n), :] = logits_of(slot, n, lax.rem(me + i + 1, 8))
             g = grad_of(lbuf[k, pl.ds(0, n), :], n, s, at, tail_at)
-            stage[out, pl.ds(0, n), :] += jnp.dot(g, zb[s], preferred_element_type=F32)
+            out[...] += jnp.dot(g, zb[s], preferred_element_type=F32)
 
         def pairs(i, _):
             one(2 * i, 0, False)
@@ -423,10 +442,65 @@
 
     gather = Gather(plane, region, gs, gr)
 
-    def keep(out, n, at):
-        return pltpu.make_async_copy(stage.at[out, pl.ds(0, n), :], de_ref.at[pl.ds(at, n), :], l_sem.at[out])
-
-    def a_step(q, _):
+    def keep(k, n, at):
+        out = stage_a.at[k] if n == A_ROWS else stage_b.at[k - A_STEPS, pl.ds(0, n), :]
+        return pltpu.make_async_copy(out, de_ref.at[pl.ds(at, n), :], l_sem.at[k])
+
+    over_tp = Exchange('tp', 4, sumbuf4, s4_s, s4_r)
+
+    def near_sums():
+        dgamma = dbeta = jnp.zeros((8, WIDTH), F32)
+        for k in range(2):
+            nears[k].wait()
+
+            def part(i, carry):
+                at = pl.multiple_of(i * 64, 64)
+                rows = pl.ds(pl.multiple_of(quarters.mine[k] + at, 64), 64)
+                dz = dzp_ref[rows, :] + half_in[k, pl.ds(at, 64), :]
+                dzh[k, pl.ds(at, 64), :] = dz
+                dzx = dz * xhat_ref[rows, :]
+                return carry[0] + jnp.sum(dzx.reshape(8, 8, WIDTH), axis=0), carry[1] + jnp.sum(dz.reshape(8, 8, WIDTH), axis=0)
+
+            dgamma, dbeta = lax.fori_loop(0, CHUNK // 64, part, (dgamma, dbeta))
+        sums[0:8, :] = dgamma
+        sums[8:16, :] = dbeta
+        over_tp.start(sums)
+        for far in fars:
+            far.start()
+        sumbuf4[tp] = sums[...]
+
+    def home(k):
+        return pltpu.make_async_copy(dhh.at[k], dh_ref.at[pl.ds(quarters.mine[k], CHUNK), :], dh_sem.at[k])
+
+    def swap_rows(k, rows):
+        return pltpu.make_async_remote_copy(
+            src_ref=dhh.at[k], dst_ref=dh_ref.at[pl.ds(rows, CHUNK), :], send_sem=dh_s.at[k], recv_sem=dh_r.at[k],
+            device_id={'tp': quarters.partner[k]}, device_id_type=MESH)
+
+    over_dp = Exchange('dp', 8, sumbuf8, s8_s, s8_r)
+
+    def far_grads():
+        over_tp.wait(sums)
+        sum4[...] = sumbuf4[0] + sumbuf4[1] + sumbuf4[2] + sumbuf4[3]
+        over_dp.start(sum4)
+        sumbuf8[me] = sum4[...]
+        for k in range(2):
+            fars[k].wait()
+
+            def part(i, _):
+                at = pl.multiple_of(i * 64, 64)
+                rows = pl.ds(pl.multiple_of(quarters.mine[k] + at, 64), 64)
+                xh = xhat_ref[rows, :]
+                g = (dzh[k, pl.ds(at, 64), :] + far_in[k, pl.ds(at, 64), :]) * gamma_ref[...]
+                g = g - jnp.mean(g, axis=-1, keepdims=True) - xh * jnp.mean(g * xh, axis=-1, keepdims=True)
+                dhh[k, pl.ds(at, 64), :] = g * inv_ref[rows, :]
+                return 0
+
+            lax.fori_loop(0, CHUNK // 64, part, 0)
+            home(k).start()
+            swap_rows(k, quarters.mine[k]).start()
+
+    def a_step(q, _, first=False):
         slot = lax.rem(q, 2)
         fetch(a_at(me, q), A_ROWS, slot).wait()
 
@@ -438,53 +512,24 @@
         def _():
             fetch(b_at(plane.core, 0), B_ROWS, 1 - slot).start()
 
-        compute(slot, 2 + q, A_ROWS, a_at(me, q))
-        keep(2 + q, A_ROWS, a_at(me, q)).start()
-        gather.send_own(q, stage.at[2 + q, pl.ds(0, A_ROWS), :])
+        if not first:
+            pl.when(q == A_STEPS - 1)(near_sums)
+        if first:
+            compute(slot, stage_a.at[q], A_ROWS, a_at(me, q), arriving=True)
+        else:
+            compute(slot, stage_a.at[q], A_ROWS, a_at(me, q))
+        keep(q, A_ROWS, a_at(me, q)).start()
+        gather.send_own(q, stage_a.at[q])
         return 0
 
-    lax.fori_loop(0, A_STEPS, a_step, 0)
-
-    over_tp.wait(sums)
-    sum4[...] = sumbuf4[0] + sumbuf4[1] + sumbuf4[2] + sumbuf4[3]
-    over_dp = Exchange('dp', 8, sumbuf8, s8_s, s8_r)
-    over_dp.start(sum4)
-    sumbuf8[me] = sum4[...]
+    a_step(0, 0, first=True)
+    lax.fori_loop(1, A_STEPS, a_step, 0)
 
     def b_copy(b, out, core):
         at = b_at(core, b)
         return pltpu.make_async_remote_copy(
-            src_ref=stage.at[out, pl.ds(0, B_ROWS), :], dst_ref=de_ref.at[pl.ds(at, B_ROWS), :],
+            src_ref=stage_b.at[out - A_STEPS, pl.ds(0, B_ROWS), :], dst_ref=de_ref.at[pl.ds(at, B_ROWS), :],
             send_sem=b_s.at[b], recv_sem=b_r.at[b], device_id={'dp': plane.pair}, device_id_type=MESH)
-
-    def b_free(b, slot):
-        @pl.when(b >= 2)
-        def _():
-            keep(slot, B_ROWS, b_at(plane.core, b - 2)).wait()
-            b_copy(b - 2, slot, plane.core).wait_send()
-
-    home = pltpu.make_async_copy(dhh, dh_ref.at[pl.ds(mine, HALF), :], dh_sem)
-    dh_pair = pltpu.make_async_remote_copy(
-        src_ref=dhh, dst_ref=dh_ref.at[pl.ds(mine, HALF), :], send_sem=dh_s, recv_sem=dh_r,
-        device_id={'tp': tp + 1 - 2 * lax.rem(tp, 2)}, device_id_type=MESH)
-    dh_from_pair = pltpu.make_async_remote_copy(
-        src_ref=dhh, dst_ref=dh_ref.at[pl.ds(pl.multiple_of(HALF - mine, HALF), HALF), :], send_sem=dh_s, recv_sem=dh_r,
-        device_id={'tp': tp + 1 - 2 * lax.rem(tp, 2)}, device_id_type=MESH)
-
-    def half_grad():
-        far.wait()
-
-        def part(i, _):
-            at = pl.multiple_of(i * 64, 64)
-            xh = xhat_ref[pl.ds(mine + at, 64), :]
-            g = (dz_ref[pl.ds(at, 64), :] + far_in[pl.ds(at, 64), :]) * gamma_ref[...]
-            g = g - jnp.mean(g, axis=-1, keepdims=True) - xh * jnp.mean(g * xh, axis=-1, keepdims=True)
-            dhh[pl.ds(at, 64), :] = g * inv_ref[pl.ds(mine + at, 64), :]
-            return 0
-
-        lax.fori_loop(0, HALF // 64, part, 0)
-        home.start()
-        dh_pair.start()
 
     def b_step(b, _):
         slot = lax.rem(b, 2)
@@ -499,51 +544,47 @@
         def _():
             fetch(b_at(plane.core, B_STEPS - 1), B_ROWS, 2).start()
 
-        @pl.when(lax.rem(b, 2) == 0)
-        def _():
-            gather.forward(lax.div(b, 2))
-
-        @pl.when(b == 5)
-        def _():
-            half_grad()
-
-        b_free(b, slot)
-        compute(slot, slot, B_ROWS, at)
-        keep(slot, B_ROWS, at).start()
-        b_copy(b, slot, plane.core).start()
+        @pl.when(lax.rem(b, B_STEPS // 4) == 0)
+        def _():
+            gather.forward(lax.div(b, B_STEPS // 4))
+
+        pl.when(b == B_STEPS // 2)(far_grads)
+        compute(slot, stage_b.at[b, pl.ds(0, B_ROWS), :], B_ROWS, at)
+        keep(A_STEPS + b, B_ROWS, at).start()
+        b_copy(b, A_STEPS + b, plane.core).start()
         return 0
 
     lax.fori_loop(0, B_STEPS - 1, b_step, 0)
 
-    b, slot = B_STEPS - 1, (B_STEPS - 1) % 2
+    b, slot = B_STEPS - 1, A_STEPS + B_STEPS - 1
     at = b_at(plane.core, b)
     fetch(at, B_ROWS, 2).wait()
     tail.wait()
+    if B_STEPS == 4:
+        gather.forward(3)
     gather.forward_diag(0)
     gather.forward_diag(1)
-    b_free(b, slot)
-    compute(2, slot, R_MAX, at, TAIL_AT)
+    compute(2, stage_b.at[b], R_MAX, at, TAIL_AT)
     keep(slot, B_ROWS, at).start()
     b_copy(b, slot, plane.core).start()
-    keep_tail = pltpu.make_async_copy(stage.at[slot, pl.ds(B_ROWS, TAIL), :], de_ref.at[pl.ds(TAIL_AT, TAIL), :], t_sem)
+    keep_tail = pltpu.make_async_copy(stage_b.at[b, pl.ds(B_ROWS, TAIL), :], de_ref.at[pl.ds(TAIL_AT, TAIL), :], t_sem)
     keep_tail.start()
 
     over_dp.wait(sum4)
     sums_out[...] = jnp.sum(sumbuf8[...], axis=0)
     for q in range(2, A_STEPS):
         gather.forward_diag(q)
-    keep(1 - slot, B_ROWS, b_at(plane.core, b - 1)).wait()
-    b_copy(b - 1, 1 - slot, plane.core).wait_send()
-    keep(slot, B_ROWS, at).wait()
     keep_tail.wait()
-    b_copy(b, slot, plane.core).wait_send()
     for k in range(B_STEPS):
-        b_copy(k, 0, 1 - plane.core).wait_recv()
-    home.wait()
-    dh_pair.wait_send()
-    dh_from_pair.wait_recv()
+        keep(A_STEPS + k, B_ROWS, b_at(plane.core, k)).wait()
+        b_copy(k, A_STEPS + k, plane.core).wait_send()
+        b_copy(k, A_STEPS + k, 1 - plane.core).wait_recv()
+    for k in range(2):
+        home(k).wait()
+        swap_rows(k, quarters.mine[k]).wait_send()
+        swap_rows(k, quarters.theirs[k]).wait_recv()
     for q in range(A_STEPS):
-        keep(2 + q, A_ROWS, a_at(me, q)).wait()
+        keep(q, A_ROWS, a_at(me, q)).wait()
         gather.own_sent(q)
         gather.finish(q)
 
@@ -574,13 +615,16 @@
             pl.BlockSpec(memory_space=pltpu.VMEM),
         ),
         scratch_shapes=[
-            pltpu.VMEM((HALF, WIDTH), F32),
-            pltpu.VMEM((HALF, WIDTH), F32),
+            pltpu.VMEM((2, CHUNK, WIDTH), F32),
+            pltpu.VMEM((2, CHUNK, WIDTH), F32),
+            pltpu.VMEM((2, CHUNK, WIDTH), F32),
+            pltpu.VMEM((2, CHUNK, WIDTH), F32),
             pltpu.VMEM((8, SEQ, WIDTH), BF16),
-            pltpu.VMEM((4, CHUNK, WIDTH), F32),
+            pltpu.VMEM((Z_SLOTS, CHUNK, WIDTH), F32),
             pltpu.VMEM((3, R_MAX + 8, WIDTH), BF16),
             pltpu.VMEM((2, R_MAX, SEQ), F32),
-            pltpu.VMEM((2 + A_STEPS, R_MAX, WIDTH), F32),
+            pltpu.VMEM((A_STEPS, A_ROWS, WIDTH), F32),
+            pltpu.VMEM((B_STEPS, R_MAX, WIDTH), F32),
             pltpu.VMEM((8, 8, SEQ), F32),
             pltpu.VMEM((8, 8, SEQ), F32),
             pltpu.VMEM((8, 8, SEQ), jnp.int32),
@@ -588,15 +632,17 @@
             pltpu.VMEM((16, WIDTH), F32),
             pltpu.VMEM((4, 16, WIDTH), F32),
             pltpu.VMEM((8, 16, WIDTH), F32),
-            pltpu.SemaphoreType.DMA,
-            pltpu.SemaphoreType.DMA,
-            pltpu.SemaphoreType.DMA,
-            pltpu.SemaphoreType.DMA,
-            pltpu.SemaphoreType.DMA,
-            pltpu.SemaphoreType.DMA((4,)),
+            pltpu.SemaphoreType.DMA((2,)),
+            pltpu.SemaphoreType.DMA((2,)),
+            pltpu.SemaphoreType.DMA((2,)),
+            pltpu.SemaphoreType.DMA((2,)),
+            pltpu.SemaphoreType.DMA((2,)),
+            pltpu.SemaphoreType.DMA((2,)),
+            pltpu.SemaphoreType.DMA((2,)),
+            pltpu.SemaphoreType.DMA((Z_SLOTS,)),
             pltpu.SemaphoreType.DMA((3,)),
             pltpu.SemaphoreType.DMA,
-            pltpu.SemaphoreType.DMA((2 + A_STEPS,)),
+            pltpu.SemaphoreType.DMA((A_STEPS + B_STEPS,)),
             pltpu.SemaphoreType.DMA((7, A_STEPS)),
             pltpu.SemaphoreType.DMA((7, A_STEPS)),
             pltpu.SemaphoreType.DMA((B_STEPS,)),
@@ -606,7 +652,7 @@
             pltpu.SemaphoreType.DMA((8,)),
             pltpu.SemaphoreType.DMA((8,)),
         ],
-        compiler_params=pltpu.CompilerParams(collective_id=2, has_side_effects=True, vmem_limit_bytes=60_000_000),
+        compiler_params=pltpu.CompilerParams(collective_id=2, has_side_effects=True, vmem_limit_bytes=VMEM_LIMIT),
         cost_estimate=pl.CostEstimate(flops=32 * SEQ * 3200 * WIDTH, bytes_accessed=8 * ROWS * WIDTH, transcendentals=8 * SEQ * 3200),
     )(z, zall, embed, info, lse, dz, xhat, inv_std, gamma)
 
@@ -619,8 +665,8 @@
         here = labels - shard_start
         here = jnp.where((here >= 0) & (here < ROWS), here, -1)
         info = jnp.concatenate([labels.astype(F32), loss_mask.astype(F32), here.astype(F32), jnp.zeros((5, SEQ), F32)], axis=0)
-        zall, dz_half, info_all, lse_all = own_tokens(z, z.astype(F32), embed_shard, info)
-        d_embed, d_rows, sums = all_tokens(z, zall, embed_shard, info_all, lse_all, dz_half, x_hat, inv_std, ln_gamma[None])
+        zall, dz_part, info_all, lse_all = own_tokens(z, z.astype(F32), embed_shard, info)
+        d_embed, d_rows, sums = all_tokens(z, zall, embed_shard, info_all, lse_all, dz_part, x_hat, inv_std, ln_gamma[None])
         mask = info_all[:, 1, :]
         mean_loss = jnp.sum(mask * (lse_all[:, 0, :] - lse_all[:, 1, :])) / jnp.sum(mask)
         d_gamma = jnp.sum(sums[:8], axis=0)

time: 327 us -> 276 us (0.84)
  Pallas kernels: 277 us -> 227 us
    pallas_call x1, Pallas kernels: 157 us -> 127 us  [all_tokens(): pl.pallas_call(all_tokens_kernel, name='all_tokens', out_shape=(jax.Shape...]
    pallas_call x1, Pallas kernels: 120 us -> 99.2 us  [own_tokens(): pl.pallas_call(own_tokens_kernel, name='own_tokens', out_shape=(jax.Shape...]
where the time goes in v2:
time: 276 us; the launch traced here: 274 us
  Pallas kernels  227 us (82%)
  local copies, waits for them, and re-layouts  29.8 us (11%)
  other arithmetic  14.6 us (5%)
  between operations  3.21 us (1%)
    pallas_call x1, Pallas kernels, all_tokens(): pl.pallas_call(all_tokens_kernel, name='all_tokens', out_shape=(jax.Shape...  127 us
    pallas_call x1, Pallas kernels, own_tokens(): pl.pallas_call(own_tokens_kernel, name='own_tokens', out_shape=(jax.Shape...  99.2 us
    unnamed x11, local copies, waits for them, and re-layouts  27.3 us

profile of v2, /device:TPU:0, one launch (start us, length us, event | category | flops | bytes accessed | tf_op | source)
XLA Modules:
  0.0 274.1 jit_solution(4963168742787623801)
XLA Ops:
  0.6 0.0 copy-start
  0.6 0.0 copy-start.2
  0.7 0.0 copy-start.4
  0.7 0.0 copy-start.3
  0.7 0.1 pad.3.clone
  0.8 1.4 broadcast_in_dim.19.gamma_ref
  2.1 0.7 convert_element_type.29
  2.8 1.7 convert_reduce_fusion
  4.5 2.0 fusion.3
  6.5 0.0 copy-done.4
  6.6 0.7 maximum_maximum_fusion.info_ref
  7.3 1.1 copy.11.inv_ref
  8.3 0.0 copy-done
  8.3 0.0 copy-done.2
  8.3 0.0 copy-done.3
  8.3 3.9 %fusion.5 = (f32[1024,768]{1,0:T(8,128)}, bf16[1024,768]{1,0:T(8,128)(2,1)}, f32[1024,768]{1,0:T(8,128)}) fusion(f32[768]{0:T(1024)S(1)} %copy-done.3, f32[768]{0:T(1024)S(1)} %copy-done.2, f32[1024]{0:T(1024)S(1)} %add_rsqrt_fusion, f32[1024]{0:T(1024)S(1)} %broadcast_multiply_fusion, bf16[1,1024,768]{2,1,0:T(8,128)(2,1)S(1)} %copy-done), kind=kLoop, calls=%fused_computation.17 | loop fusion | flops 5505024 | bytes 9451520 | tf_op jit(solution)/shard_map/convert_element_type | solution.py:668
  12.2 99.2 %own_tokens.1 = (f32[8,1024,768]{2,1,0:T(8,128)}, f32[1024,768]{1,0:T(8,128)}, f32[8,8,1024]{2,1,0:T(8,128)}, f32[8,8,1024]{2,1,0:T(8,128)}) custom-call(bf16[1024,768]{1,0:T(8,128)(2,1)} %get-tuple-element.24.z_ref, f32[1024,768]{1,0:T(8,128)} %get-tuple-element.23.zf_ref, bf16[12568,768]{1,0:T(8,128)(2,1)} %e_ref.3, f32[8,1024]{1,0:T(8,128)} %maximum_maximum_fusion.info_ref), custom_call_target="tpu_custom_call" | custom-call | flops 39535509504 | bytes 38608896 | tf_op jit(solution)/shard_map/own_tokens/pallas_call | solution.py:297
  111.4 1.8 slice_reduce_fusion.2
  114.5 127.3 %all_tokens.1 = (f32[12568,768]{1,0:T(8,128)}, f32[1024,768]{1,0:T(8,128)}, f32[16,768]{1,0:T(8,128)}) custom-call(bf16[1024,768]{1,0:T(8,128)(2,1)} %get-tuple-element.24.z_ref, f32[8,1024,768]{2,1,0:T(8,128)} %get-tuple-element.14.zall_ref, bf16[12568,768]{1,0:T(8,128)(2,1)} %e_ref.3, f32[8,8,1024]{2,1,0:T(8,128)} %get-tuple-element.12.info_ref, ...), custom_call_target="tpu_custom_call" | custom-call | flops 80530636800 | bytes 77217792 | tf_op jit(solution)/shard_map/all_tokens/pallas_call | solution.py:593
  241.9 0.0 copy-start.1
  241.9 3.2 %convert_bitcast_fusion.1 = bf16[1,1024,768]{2,1,0:T(8,128)(2,1)} fusion(f32[1024,768]{1,0:T(8,128)} %get-tuple-element.16), kind=kLoop, calls=%fused_computation.7 | loop fusion | flops 786432 | bytes 4718592 | tf_op jit(solution)/shard_map/broadcast_in_dim | solution.py:674
  245.1 0.0 copy-done.1
  245.1 0.6 slice_reduce_fusion
  245.7 27.3 %copy.13 = f32[12568,768]{1,0:T(8,128)} copy(f32[12568,768]{1,0:T(8,128)} %get-tuple-element.35) | data formatting | bytes 77217792
  (4 shorter events, 0.0 us)
Async XLA Ops:
  0.6 7.7 %copy-start = (bf16[1,1024,768]{2,1,0:T(8,128)(2,1)S(1)}, bf16[1,1024,768]{2,1,0:T(8,128)(2,1)}, u32[]{:S(2)}) copy-start(bf16[1,1024,768]{2,1,0:T(8,128)(2,1)} %param.6) | copy-start | bytes 4718596
  0.6 7.7 %copy-start.2 = (f32[768]{0:T(1024)S(1)}, f32[768]{0:T(1024)}, u32[]{:S(2)}) copy-start(f32[768]{0:T(1024)} %param.7) | copy-start | bytes 9220
  0.7 5.9 %copy-start.4 = (s32[1,1024]{1,0:T(1,128)S(1)}, s32[1,1024]{1,0:T(1,128)}, u32[]{:S(2)}) copy-start(s32[1,1024]{1,0:T(1,128)} %param.10) | copy-start | bytes 12292
  0.7 7.7 %copy-start.3 = (f32[768]{0:T(1024)S(1)}, f32[768]{0:T(1024)}, u32[]{:S(2)}) copy-start(f32[768]{0:T(1024)} %param.8) | copy-start | bytes 9220
  241.9 3.2 %copy-start.1 = (f32[16,768]{1,0:T(8,128)S(1)}, f32[16,768]{1,0:T(8,128)}, u32[]{:S(2)}) copy-start(f32[16,768]{1,0:T(8,128)} %get-tuple-element.18) | copy-start | bytes 147460

commit v3 on v2

--- a/solution.py
+++ b/solution.py
@@ -544,9 +544,8 @@
         def _():
             fetch(b_at(plane.core, B_STEPS - 1), B_ROWS, 2).start()
 
-        @pl.when(lax.rem(b, B_STEPS // 4) == 0)
-        def _():
-            gather.forward(lax.div(b, B_STEPS // 4))
+        gather.forward(b)
+        pl.when(b == B_STEPS - 2)(lambda: gather.forward(b + 1))
 
         pl.when(b == B_STEPS // 2)(far_grads)
         compute(slot, stage_b.at[b, pl.ds(0, B_ROWS), :], B_ROWS, at)
@@ -560,8 +559,6 @@
     at = b_at(plane.core, b)
     fetch(at, B_ROWS, 2).wait()
     tail.wait()
-    if B_STEPS == 4:
-        gather.forward(3)
     gather.forward_diag(0)
     gather.forward_diag(1)
     compute(2, stage_b.at[b], R_MAX, at, TAIL_AT)

time: 276 us -> 276 us (level)
  no operation moved by 1% of the time
where the time goes in v3:
time: 276 us; the launch traced here: 274 us
  Pallas kernels  227 us (82%)
  local copies, waits for them, and re-layouts  29.8 us (11%)
  other arithmetic  14.6 us (5%)
  between operations  3.21 us (1%)
    pallas_call x1, Pallas kernels, all_tokens(): pl.pallas_call(all_tokens_kernel, name='all_tokens', out_shape=(jax.Shape...  127 us
    pallas_call x1, Pallas kernels, own_tokens(): pl.pallas_call(own_tokens_kernel, name='own_tokens', out_shape=(jax.Shape...  99.2 us
    unnamed x11, local copies, waits for them, and re-layouts  27.3 us

profile of v3, /device:TPU:0, one launch (start us, length us, event | category | flops | bytes accessed | tf_op | source)
XLA Modules:
  0.0 274.1 jit_solution(3025695570851482369)
XLA Ops:
  0.6 0.0 copy-start
  0.6 0.0 copy-start.2
  0.7 0.0 copy-start.4
  0.7 0.0 copy-start.3
  0.7 0.1 pad.3.clone
  0.8 1.4 broadcast_in_dim.19.gamma_ref
  2.1 0.7 convert_element_type.29
  2.8 1.7 convert_reduce_fusion
  4.5 2.0 fusion.3
  6.5 0.0 copy-done.4
  6.6 0.7 maximum_maximum_fusion.info_ref
  7.3 1.1 copy.11.inv_ref
  8.3 0.0 copy-done
  8.3 0.0 copy-done.2
  8.3 0.0 copy-done.3
  8.3 3.9 %fusion.5 = (f32[1024,768]{1,0:T(8,128)}, bf16[1024,768]{1,0:T(8,128)(2,1)}, f32[1024,768]{1,0:T(8,128)}) fusion(f32[768]{0:T(1024)S(1)} %copy-done.3, f32[768]{0:T(1024)S(1)} %copy-done.2, f32[1024]{0:T(1024)S(1)} %add_rsqrt_fusion, f32[1024]{0:T(1024)S(1)} %broadcast_multiply_fusion, bf16[1,1024,768]{2,1,0:T(8,128)(2,1)S(1)} %copy-done), kind=kLoop, calls=%fused_computation.17 | loop fusion | flops 5505024 | bytes 9451520 | tf_op jit(solution)/shard_map/convert_element_type | solution.py:665
  12.2 99.2 %own_tokens.1 = (f32[8,1024,768]{2,1,0:T(8,128)}, f32[1024,768]{1,0:T(8,128)}, f32[8,8,1024]{2,1,0:T(8,128)}, f32[8,8,1024]{2,1,0:T(8,128)}) custom-call(bf16[1024,768]{1,0:T(8,128)(2,1)} %get-tuple-element.24.z_ref, f32[1024,768]{1,0:T(8,128)} %get-tuple-element.23.zf_ref, bf16[12568,768]{1,0:T(8,128)(2,1)} %e_ref.3, f32[8,1024]{1,0:T(8,128)} %maximum_maximum_fusion.info_ref), custom_call_target="tpu_custom_call" | custom-call | flops 39535509504 | bytes 38608896 | tf_op jit(solution)/shard_map/own_tokens/pallas_call | solution.py:297
  111.4 1.8 slice_reduce_fusion.2
  114.5 127.3 %all_tokens.1 = (f32[12568,768]{1,0:T(8,128)}, f32[1024,768]{1,0:T(8,128)}, f32[16,768]{1,0:T(8,128)}) custom-call(bf16[1024,768]{1,0:T(8,128)(2,1)} %get-tuple-element.24.z_ref, f32[8,1024,768]{2,1,0:T(8,128)} %get-tuple-element.14.zall_ref, bf16[12568,768]{1,0:T(8,128)(2,1)} %e_ref.3, f32[8,8,1024]{2,1,0:T(8,128)} %get-tuple-element.12.info_ref, ...), custom_call_target="tpu_custom_call" | custom-call | flops 80530636800 | bytes 77217792 | tf_op jit(solution)/shard_map/all_tokens/pallas_call | solution.py:590
  241.9 0.0 copy-start.1
  241.9 3.2 %convert_bitcast_fusion.1 = bf16[1,1024,768]{2,1,0:T(8,128)(2,1)} fusion(f32[1024,768]{1,0:T(8,128)} %get-tuple-element.16), kind=kLoop, calls=%fused_computation.7 | loop fusion | flops 786432 | bytes 4718592 | tf_op jit(solution)/shard_map/broadcast_in_dim | solution.py:671
  245.1 0.0 copy-done.1
  245.1 0.6 slice_reduce_fusion
  245.7 27.3 %copy.13 = f32[12568,768]{1,0:T(8,128)} copy(f32[12568,768]{1,0:T(8,128)} %get-tuple-element.35) | data formatting | bytes 77217792
  (4 shorter events, 0.0 us)
Async XLA Ops:
  0.6 7.7 %copy-start = (bf16[1,1024,768]{2,1,0:T(8,128)(2,1)S(1)}, bf16[1,1024,768]{2,1,0:T(8,128)(2,1)}, u32[]{:S(2)}) copy-start(bf16[1,1024,768]{2,1,0:T(8,128)(2,1)} %param.6) | copy-start | bytes 4718596
  0.6 7.7 %copy-start.2 = (f32[768]{0:T(1024)S(1)}, f32[768]{0:T(1024)}, u32[]{:S(2)}) copy-start(f32[768]{0:T(1024)} %param.7) | copy-start | bytes 9220
  0.7 5.9 %copy-start.4 = (s32[1,1024]{1,0:T(1,128)S(1)}, s32[1,1024]{1,0:T(1,128)}, u32[]{:S(2)}) copy-start(s32[1,1024]{1,0:T(1,128)} %param.10) | copy-start | bytes 12292
  0.7 7.7 %copy-start.3 = (f32[768]{0:T(1024)S(1)}, f32[768]{0:T(1024)}, u32[]{:S(2)}) copy-start(f32[768]{0:T(1024)} %param.8) | copy-start | bytes 9220
  241.9 3.2 %copy-start.1 = (f32[16,768]{1,0:T(8,128)S(1)}, f32[16,768]{1,0:T(8,128)}, u32[]{:S(2)}) copy-start(f32[16,768]{1,0:T(8,128)} %get-tuple-element.18) | copy-start | bytes 147460
